TPU v7x, 32 devices: a 4x2x2 block of a 4x4x8 slice. The times are simulated.
32 devices in a mesh: dp: 4 (over y, z), tp: 8 (over x, core).
Axes of the slice: x: 4, y: 2, z: 2, core: 2. Of those that a mesh axis runs over, the one named last changes fastest.
The devices are a block of a 4x4x8 slice.
Arguments:
- x_seq: bfloat16 [24, 2048, 2048], P('dp', 'tp'), parts along dimension 0
- ln_gain: float32 [2048], replicated
- ln_bias: float32 [2048], replicated
- w_qkv: bfloat16 [2048, 8, 3, 256], P(None, 'tp')
- w_out: bfloat16 [2048, 2048], P('tp')
- w_up: bfloat16 [2048, 8192], P(None, 'tp')
- w_down: bfloat16 [8192, 2048], P('tp')
Outputs:
- output: bfloat16 [24, 2048, 2048], P('dp', 'tp'), parts along dimension 0
There are 4 independent parts. A program takes and returns all parts, laid end to end along the dimension named above; an argument that names none is the same for every part.
All inputs are finite; a program needn't handle non-finite values.
Results may differ from a plain program's by a relative error of at most 0.0116155.
Values are sent between devices in bfloat16 or wider.
A program may use at most 768 MiB of HBM per device.

v0:
```python
import functools

import jax
import jax.numpy as jnp
from jax import lax
from jax.experimental import pallas as pl
from jax.experimental.pallas import tpu as pltpu
from jax.sharding import PartitionSpec as P

LN_EPS = 1e-5
MESH = pl.DeviceIdType.MESH
BF16 = jnp.bfloat16
F32 = jnp.float32
LOG2E = 1.4426950408889634
VMEM_LIMIT = 67_043_328

W_Q, W_K, W_V, UP0, UP1, DN0, DN1, DN2, DN3, OUT = range(10)
PIECES = 10
FAR, MATE, PART, OWN = range(4)
TILE, ATT, UP, DOWN = range(4)
INTER = ("Q2", "Q1", "Q0", "p01", "p00", "U0", "U1", "D2", "p11", "p10", "D0", "O", "D1", "D3", "p20", "p21")
ORDER = ("A00", "A01", "A02", "A03", "T00", "T01", "T02", "T03", "A10", "A11", "U0F", "U1M",
         "U0M", "A12", "A13", "T10", "T11", "T12", "T13", "A20", "D0F", "A21", "D1M", "U1F",
         "D0M", "A22", "U0P", "D1F", "A23", "T20", "D0P", "T21", "T22", "T23", "U2F", "D2F",
         "U1P", "D1P", "U2M", "D2M", "U2P", "U1O", "D2P", "D1O", "U0O", "D0O", "U2O", "D2O",
         )
START = ("pqQ2", "pqQ1", "phQ2", "pqQ0", "phQ1", "rm0", "nm10", "phQ0", "rp01")
BEFORE = {
    0: ("ld00", "ld01"),
    2: ("rp00", "ld02"),
    3: ("pqU0", "rf0", "nm11", "pqU1", "ld03", "ln0"),
    4: ("phU0", "pqD2"),
    5: ("nm20",),
    6: ("rm1",),
    7: ("phU1", "ld10"),
    8: ("rp11", "ld11"),
    10: ("phD2", "rp10", "ln1", "ow0", "lo0"),
    11: ("pqD0", "ln2"),
    12: ("pqO", "ld12", "lo2"),
    13: ("phD0", "pqD1", "rf1", "nm21"),
    14: ("ld13", "ln3"),
    15: ("pqD3", "phO"),
    18: ("phD1", "rm2", "rp20", "ld20"),
    19: ("phD3", "ow1", "lo1"),
    20: ("rp21", "ld21"),
    22: ("ad0F",),
    23: ("rf2", "ln4", "lo3"),
    24: ("ld22",),
    26: ("lo4",),
    27: ("ld23",),
    28: ("ln5",),
    34: ("ln6", "ow2", "lo5"),
    36: ("ln7", "lo6"),
    38: ("ln8", "lo7"),
    40: ("ln9", "lo8"),
    41: ("ln10", "lo9"),
    44: ("ln11", "lo10"),
    46: ("lo11",),
}
ADDS = { 24: "1M", 29: "1F", 32: "0P", 33: "0M", 37: "2F", 39: "1P", 41: "2M", 44: "2P", 45: "1O", 47: "0O" }
LAST_ADDS = ("2O",)

KINDS = "ATUD"
BLOCKS = "FMPO"
ITEMS = tuple((int(x[1]), BLOCKS.index(x[2])) for x in ORDER if x[0] == "U")
SLOTS = 4
PIECE = {"Q0": W_Q, "Q1": W_K, "Q2": W_V, "U0": UP0, "U1": UP1,
         "D0": DN0, "D1": DN1, "D2": DN2, "D3": DN3, "O": OUT}


def code_of(step):
    what, s = KINDS.index(step[0]), int(step[1])
    return 16 * what + (4 * s + int(step[2]) if what < UP else ITEMS.index((s, BLOCKS.index(step[2]))))


def pick(values, i, bits):
    per = 30 // bits
    words = [sum(v << bits * p for p, v in enumerate(values[w:w + per])) for w in range(0, len(values), per)]
    word, at = lax.div(i, per), lax.rem(i, per)
    packed = jnp.int32(words[0])
    for w in range(1, len(words)):
        packed = jnp.where(word == w, words[w], packed)
    out = packed
    for p in range(1, per):
        out = jnp.where(at == p, lax.div(packed, 1 << bits * p), out)
    return lax.rem(out, 1 << bits)


def sums():
    seq = []
    for t in range(len(ORDER)):
        seq += [(name[2:], t) for name in BEFORE.get(t, ()) if name[:2] == "ad"]
        if t in ADDS:
            seq.append((ADDS[t], t))
    seq += [(name, None) for name in LAST_ADDS]
    last, before = {}, {}
    for name, _ in seq:
        before[name] = last.get(name[1], -1)
        last[name[1]] = int(name[0])
    assert len(seq) == len(ITEMS)
    return before, last


BEFORE_SUM, LAST_SUM = sums()


def layer_kernel(dims, x, gain, bias, w_qkv, w_out, w_up, w_dn,
                 branch, ng, nout, obuf, ownp, sibin, mid,
                 wq, wu, wd, xt, nt, qk, vt, ot, ho, stage, cin, tbuf, acc, m_s, l_s,
                 w_l, wx_s, wx_r, wf_s, wf_r, nm_s, nm_r, np_s, np_r, nf_s, nf_r, nd_s, nd_r,
                 sp_s, sp_r, op_sem, t_s, t_r, p_s, p_r,
                 ln_sem, xt_sem, oo_sem, nl_sem, ol_sem, cl_sem, br_sem):
    span, rows, d_model, head, ff, chunk, ln_rows, add_rows = dims
    half = rows // 2
    blk = 2 * rows
    scale = LOG2E * head ** -0.5

    g, me = lax.axis_index("dp"), lax.axis_index("tp")
    c, j = lax.div(me, 2), lax.rem(me, 2)
    o = 1 - j
    pair = lax.div(c, 2)
    mate = c + 1 - 2 * lax.rem(c, 2)
    part = 3 - c
    far = 3 - mate
    zb, yb = lax.rem(g, 2), lax.rem(lax.div(g, span), 2)
    gz, gy = g + 1 - 2 * zb, g + span * (1 - 2 * yb)

    def dev(chip, core, group=g):
        return {"dp": group, "tp": 2 * chip + core}

    sib, mt, pt, zd, yd = dev(c, o), dev(mate, j), dev(part, j), dev(c, j, gz), dev(c, j, gy)

    def remote(src, dst, send, recv, to):
        return pltpu.make_async_remote_copy(src_ref=src, dst_ref=dst, send_sem=send, recv_sem=recv,
                                            device_id=to, device_id_type=MESH)

    def row(chip, core, extra=0):
        return pl.multiple_of((2 * chip + core) * rows + extra, half)

    def rowblock(chip):
        return pl.ds(pl.multiple_of(chip * blk, blk), blk)

    quarter = 2 * yb + zb
    q_z, q_y, q_zy = quarter + 1 - 2 * zb, quarter + 2 - 4 * yb, 3 - quarter

    def w_at(piece, q, side, hold):
        n = head // 4 if piece == OUT else ff // 16 if piece >= DN0 else d_model // 8 if piece >= UP0 else d_model // 4
        size = n if side is None else n // 2
        off = q * n + (0 if side is None else side * size)
        if UP0 <= piece <= DN3:
            off = off + (piece - (UP0 if piece <= UP1 else DN0)) * 4 * n
        if hold and DN0 <= piece <= DN3:
            off = off + ff
        if hold and piece == OUT:
            off = off + 2 * ff + head
        at = pl.ds(pl.multiple_of(off, n // 2), size)
        if piece <= W_V:
            return wq.at[piece, at, pl.ds(head, head)] if hold else w_qkv.at[piece, at, :]
        if piece <= UP1:
            return wu.at[at, pl.ds(ff, ff)] if hold else w_up.at[at, :]
        return wd.at[at, :] if hold else (w_out if piece == OUT else w_dn).at[at, :]

    def w_own(i):
        src, dst = ((w_qkv, wq.at[:, :, pl.ds(0, head)]), (w_up, wu.at[:, pl.ds(0, ff)]),
                    (w_dn, wd.at[pl.ds(0, ff), :]), (w_out, wd.at[pl.ds(2 * ff, head), :]))[i]
        return pltpu.make_async_copy(src, dst, w_l.at[i])

    def wx(k):
        return remote(w_at(k, quarter, None, False), w_at(k, quarter, None, True), wx_s.at[k], wx_r.at[k], pt)

    def wx_in(k):
        ref = w_at(k, quarter, None, True)
        return remote(ref, ref, wx_s.at[k], wx_r.at[k], pt)

    def wf(k, i):
        ref = (w_at(k, quarter, None, True) if i < 2 else w_at(k, q_y, 1, True) if i == 2 else w_at(k, q_z, 0, True))
        return remote(ref, ref, wf_s.at[k, i], wf_r.at[k, i], yd if i in (1, 3) else zd)

    def wf_in(k, i):
        ref = w_at(k, (q_z, q_y, q_zy, q_zy)[i], (None, None, 1, 0)[i], True)
        return remote(ref, ref, wf_s.at[k, i], wf_r.at[k, i], yd if i in (1, 3) else zd)

    def pass_quarter(k):
        wx_in(k).wait_recv()
        wf(k, 0).start()
        wf(k, 1).start()

    def pass_halves(k):
        wf_in(k, 0).wait_recv()
        wf_in(k, 1).wait_recv()
        wf(k, 2).start()
        wf(k, 3).start()

    def have(k):
        wf_in(k, 2).wait_recv()
        wf_in(k, 3).wait_recv()

    def own_seq(s):
        return 2 * s + pair

    def other_seq(s):
        return 2 * s + 1 - pair

    def n_own(s):
        return ng.at[s, pl.ds(row(c, j), rows)]

    def nm(s, h):
        ref = ng.at[s, pl.ds(row(c, j, h * half), half)]
        return remote(ref, ref, nm_s.at[s, h], nm_r.at[s, h], mt)

    def nm_in(s, h):
        ref = ng.at[s, pl.ds(row(mate, j, h * half), half)]
        return remote(ref, ref, nm_s.at[s, h], nm_r.at[s, h], mt)

    def np_(s, h):
        return remote(nout.at[s, pl.ds(h * half, half)], ng.at[s, pl.ds(row(c, j, h * half), half)],
                      np_s.at[s, h], np_r.at[s, h], pt)

    def np_in(s, h):
        ref = ng.at[s, pl.ds(row(part, j, h * half), half)]
        return remote(ref, ref, np_s.at[s, h], np_r.at[s, h], pt)

    def nf(s, h):
        ref = ng.at[s, pl.ds(row(part, j, h * half), half)]
        return remote(ref, ref, nf_s.at[s, h], nf_r.at[s, h], mt)

    def nf_in(s, h):
        ref = ng.at[s, pl.ds(row(far, j, h * half), half)]
        return remote(ref, ref, nf_s.at[s, h], nf_r.at[s, h], mt)

    def nd(s, i, core=j):
        ref = (ng.at[s, pl.ds(row(c if i == 0 else mate, core), rows)] if i < 2 else
               ng.at[s, pl.ds(row(part if i < 4 else far, core, (i % 2) * half), half)])
        return remote(ref, ref, nd_s.at[s, i], nd_r.at[s, i], sib)

    def nd_in(s, i):
        return nd(s, i, o)

    def relay_mate(s):
        for h in range(2):
            nm_in(s, h).wait_recv()
        nd(s, 1).start()

    def relay_part(s, h):
        np_in(s, h).wait_recv()
        nf(s, h).start()
        nd(s, 2 + h).start()

    def relay_far(s):
        for h in range(2):
            nf_in(s, h).wait_recv()
            nd(s, 4 + h).start()

    def ln_buf(b):
        return (xt if b < 4 else nt).at[(b // 2) % 2, pl.ds((b % 2) * rows, rows)]

    def ln_load(b):
        return pltpu.make_async_copy(x.at[own_seq(b // 2) if b % 2 else other_seq(b // 2)], ln_buf(b), ln_sem.at[b])

    def ln_store(b):
        return pltpu.make_async_copy(ln_buf(b), n_own(b // 2) if b % 2 else nout.at[b // 2], ln_sem.at[b])

    def normalise(b):
        ln_load(b).wait()
        buf = ln_buf(b)

        def norm(r, _):
            rr = pl.ds(pl.multiple_of(r * ln_rows, ln_rows), ln_rows)
            v = buf[rr, :].astype(F32)
            mean = jnp.mean(v, axis=-1, keepdims=True)
            cen = v - mean
            var = jnp.mean(cen * cen, axis=-1, keepdims=True)
            buf[rr, :] = (cen * lax.rsqrt(var + LN_EPS) * gain[...] + bias[...]).astype(BF16)
            return 0

        lax.fori_loop(0, rows // ln_rows, norm, 0)
        ln_store(b).start()

    barrier = pltpu.get_barrier_semaphore()
    for to in (sib, mt, pt, zd, yd):
        pl.semaphore_signal(barrier, inc=1, device_id=to, device_id_type=MESH)
    for b in range(6):
        ln_load(b).start()
    pl.semaphore_wait(barrier, 5)

    first = next(i for i, name in enumerate(INTER) if name[0] == "p")
    for name in INTER[:first]:
        wx(PIECE[name]).start()
    normalise(0)
    normalise(1)
    begun = set()
    for name in INTER[first:]:
        if name[0] != "p":
            wx(PIECE[name]).start()
            continue
        s, h = int(name[1]), int(name[2])
        if s not in begun:
            if s > 0:
                normalise(2 * s)
                normalise(2 * s + 1)
            ln_store(2 * s).wait()
        np_(s, h).start()
        if s == 0 and s not in begun:
            ln_store(1).wait()
            nm(0, 0).start()
            nm(0, 1).start()
            nd(0, 0).start()
        begun.add(s)
    for s in (1, 2):
        ln_store(2 * s + 1).wait()
        nd(s, 0).start()

    def tile_chip(i):
        return jnp.where(i == 0, c, jnp.where(i == 1, mate, jnp.where(i == 2, part, far)))

    def mlp_chip(kind):
        return jnp.where(kind == FAR, far, jnp.where(kind == MATE, mate, jnp.where(kind == PART, part, c)))

    def tile_copy(s, i):
        return pltpu.make_async_copy(ng.at[s, rowblock(tile_chip(i))], xt.at[lax.rem(i, 2)], xt_sem.at[lax.rem(i, 2)])

    def tile_start(s, i):
        for n in ((0,), (1,), (2, 3), (4, 5))[i]:
            nd_in(s, n).wait_recv()
        tile_copy(s, jnp.int32(i)).start()

    def tile(index):
        s, i = lax.div(index, 4), lax.rem(index, 4)
        tile_copy(s, i).wait()
        slot = lax.rem(i, 2)
        base = rowblock(tile_chip(i))
        for t in range(2):
            qk[base, pl.ds(t * 2 * head, 2 * head)] = jnp.dot(
                xt[slot], wq[t], preferred_element_type=F32).astype(BF16)
        vt[:, base] = jnp.transpose(jnp.dot(xt[slot], wq[2], preferred_element_type=F32)).astype(BF16)

    def dot_t(a, b):
        return lax.dot_general(a, b, (((1,), (1,)), ((), ())), preferred_element_type=F32)

    def o_out(s, i):
        return pltpu.make_async_copy(ot.at[lax.rem(i, 2)], obuf.at[s, rowblock(i)], oo_sem.at[lax.rem(i, 2)])

    def attend(index):
        s, i = lax.div(index, 4), lax.rem(index, 4)
        slot = lax.rem(i, 2)

        @pl.when(i >= 2)
        def _():
            o_out(s, i).wait()

        mine = rowblock(i)
        causal = (lax.broadcasted_iota(jnp.int32, (blk, blk), 0)
                  <= lax.broadcasted_iota(jnp.int32, (blk, blk), 1))
        for h in range(2):
            hd = pl.ds(h * head, head)
            sc = jnp.where(causal, dot_t(qk[mine, pl.ds((2 + h) * head, head)], qk[mine, hd]), -jnp.inf)
            top = jnp.max(sc, axis=0, keepdims=True)
            p = jnp.exp2((sc - top) * scale)
            m_s[h] = top
            l_s[h] = jnp.sum(p, axis=0, keepdims=True)
            acc[h] = jnp.dot(vt[hd, mine], p.astype(BF16), preferred_element_type=F32)

        def earlier(t, _):
            there = rowblock(t)
            for h in range(2):
                hd = pl.ds(h * head, head)
                sc = dot_t(qk[there, pl.ds((2 + h) * head, head)], qk[mine, hd])
                old = m_s[h]
                top = jnp.maximum(old, jnp.max(sc, axis=0, keepdims=True))
                p = jnp.exp2((sc - top) * scale)
                fade = jnp.exp2((old - top) * scale)
                m_s[h] = top
                l_s[h] = l_s[h] * fade + jnp.sum(p, axis=0, keepdims=True)
                acc[h] = acc[h] * fade + jnp.dot(vt[hd, there], p.astype(BF16), preferred_element_type=F32)
            return 0

        lax.fori_loop(0, i, earlier, 0)
        for h in range(2):
            ot[slot, :, pl.ds(h * head, head)] = jnp.transpose(acc[h] * (1.0 / l_s[h])).astype(BF16)
        o_out(s, i).start()

    def context_out(s):
        for i in (2, 3):
            o_out(jnp.int32(s), jnp.int32(i)).wait()

    def sp(s, kind, slot):
        return remote(stage.at[slot, pl.ds(pl.multiple_of(o * rows, rows), rows)], sibin.at[s, kind],
                      sp_s.at[s, kind], sp_r.at[s, kind], sib)

    def own_store(s, kind, slot):
        return pltpu.make_async_copy(stage.at[slot, pl.ds(pl.multiple_of(j * rows, rows), rows)], ownp.at[s, kind],
                                     op_sem.at[slot])

    def to_mate(s, kind):
        return remote(tbuf.at[kind], mid.at[s, kind], t_s.at[s, kind], t_r.at[s, kind], mt)

    def from_mate(s, kind):
        return remote(mid.at[s, kind], mid.at[s, kind], t_s.at[s, kind], t_r.at[s, kind], mt)

    def to_part(s):
        return remote(tbuf.at[PART], branch.at[own_seq(s)], p_s.at[s], p_r.at[s], pt)

    def from_part(s):
        return remote(branch.at[other_seq(s)], branch.at[other_seq(s)], p_s.at[s], p_r.at[s], pt)

    def keep(s):
        return pltpu.make_async_copy(tbuf.at[OWN], branch.at[own_seq(s)], br_sem)

    def sent(s, kind):
        if kind < PART:
            to_mate(s, kind).wait_send()
        elif kind == PART:
            to_part(s).wait_send()
        else:
            keep(s).wait()

    def add_now(name):
        s, kind = jnp.int32(int(name[0])), BLOCKS.index(name[1])
        add_start(s, kind, jnp.int32(BEFORE_SUM[name]))
        add_finish(s, kind)

    def add_loads(s, kind):
        srcs = [ownp.at[s, kind], sibin.at[s, kind]] + ([mid.at[s, kind - PART]] if kind >= PART else [])
        return [pltpu.make_async_copy(src, cin.at[n], cl_sem.at[n]) for n, src in enumerate(srcs)]

    def add_start(s, kind, before):
        remote(sibin.at[s, kind], sibin.at[s, kind], sp_s.at[s, kind], sp_r.at[s, kind], sib).wait_recv()
        if kind >= PART:
            from_mate(s, kind - PART).wait_recv()

        @pl.when(before >= 0)
        def _():
            sent(before, kind)

        for ld in add_loads(s, kind):
            ld.start()

    def add_finish(s, kind):
        for ld in add_loads(s, kind):
            ld.wait()

        def add(r, _):
            rr = pl.ds(pl.multiple_of(r * add_rows, add_rows), add_rows)
            if kind < PART:
                tbuf[kind, rr, :] = cin[0, rr, :] + cin[1, rr, :]
            else:
                tbuf[kind, rr, :] = (cin[0, rr, :].astype(F32) + cin[1, rr, :].astype(F32)
                                     + cin[2, rr, :].astype(F32)).astype(BF16)
            return 0

        lax.fori_loop(0, rows // add_rows, add, 0)
        if kind < PART:
            to_mate(s, kind).start()
        elif kind == PART:
            to_part(s).start()
        else:
            keep(s).start()

    def item(k):
        both = pick([4 * s + b for s, b in ITEMS], k, 4)
        return lax.div(both, 4), lax.rem(both, 4)

    def n_load(k):
        s, kind = item(k)
        return pltpu.make_async_copy(ng.at[s, rowblock(mlp_chip(kind))], nt.at[lax.rem(k, 2)], nl_sem.at[lax.rem(k, 2)])

    def o_load(k):
        s, kind = item(k)
        return pltpu.make_async_copy(obuf.at[s, rowblock(mlp_chip(kind))],
                                     ho.at[lax.rem(k, SLOTS), :, pl.ds(2 * ff, 2 * head)], ol_sem.at[lax.rem(k, SLOTS)])

    def mlp_up(k):
        n_load(k).wait()

        @pl.when(k == 0)
        def _():
            have(UP0)
            have(UP1)
            w_own(1).wait()

        src, dst = lax.rem(k, 2), lax.rem(k, SLOTS)

        def up(t, _):
            cols = pl.ds(pl.multiple_of(t * chunk, chunk), chunk)
            hid = jnp.dot(nt[src], wu[:, cols], preferred_element_type=F32)
            ho[dst, :, cols] = (0.5 * hid * (1.0 + lax.erf(hid * 0.7071067811865476))).astype(BF16)
            return 0

        lax.fori_loop(0, 2 * ff // chunk, up, 0, unroll=True)

    def stage_free(k):
        s, kind = item(k)
        sp(s, kind, lax.rem(k, 2)).wait_send()

    def own_stored(k):
        s, kind = item(k)
        own_store(s, kind, lax.rem(k, 2)).wait()

    def mlp_down(k):
        s, kind = item(k)
        slot, src = lax.rem(k, 2), lax.rem(k, SLOTS)
        o_load(k).wait()

        @pl.when(k == 0)
        def _():
            for p in range(DN0, OUT + 1):
                have(p)
            w_own(2).wait()
            w_own(3).wait()

        @pl.when(k >= 2)
        def _():
            stage_free(k - 2)

        def down(r, size):
            def one(t, _):
                cols = pl.ds(pl.multiple_of(t * chunk, chunk), chunk)
                stage[slot, pl.ds(r, size), cols] = jnp.dot(
                    ho[src, pl.ds(r, size), :], wd[:, cols], preferred_element_type=F32).astype(BF16)
                return 0

            lax.fori_loop(0, d_model // chunk, one, 0, unroll=True)

        split = (k == 0) | (k == len(ITEMS) - 1)

        @pl.when(jnp.logical_not(split))
        def _():
            down(0, blk)
            sp(s, kind, slot).start()

        @pl.when(split)
        def _():
            def part_of(p, _):
                down(pl.multiple_of(jnp.where(p == 0, o, j) * rows, rows), rows)

                @pl.when(p == 0)
                def _():
                    sp(s, kind, slot).start()

                return 0

            lax.fori_loop(0, 2, part_of, 0)

        own_store(s, kind, slot).start()

    def act(name):
        what, arg = name[:2], name[2:]
        if what == "pq":
            pass_quarter(PIECE[arg])
        elif what == "ph":
            pass_halves(PIECE[arg])
        elif what == "rm":
            relay_mate(int(arg))
        elif what == "rp":
            relay_part(int(arg[0]), int(arg[1]))
        elif what == "rf":
            relay_far(int(arg))
        elif what == "ld":
            tile_start(int(arg[0]), int(arg[1]))
        elif what == "nm":
            nm(int(arg[0]), int(arg[1])).start()
        elif what == "ad":
            add_now(arg)
        elif what == "ow":
            context_out(int(arg))
        elif what == "ln":
            n_load(jnp.int32(int(arg))).start()
        else:
            o_load(jnp.int32(int(arg))).start()

    for i in range(4):
        w_own(i).start()
    for name in START:
        act(name)
    w_own(0).wait()
    for k in (W_Q, W_K, W_V):
        have(k)

    codes = [code_of(step) for step in ORDER]

    def add_code(name):
        return 1 + 4 * int(name[0]) + BLOCKS.index(name[1]) + 12 * (1 + BEFORE_SUM[name])

    adds = [add_code(ADDS[t]) if t in ADDS else 0 for t in range(len(ORDER))]

    def adding(code, do):
        @pl.when(code > 0)
        def _():
            which = lax.rem(code - 1, 12)
            for kind in range(4):
                @pl.when(lax.rem(which, 4) == kind)
                def _(kind=kind):
                    do(lax.div(which, 4), kind, lax.div(code - 1, 12) - 1)

    def events(t, lo, size):
        if not any(p in BEFORE for p in range(lo, lo + size)):
            return
        if size == 1:
            for name in BEFORE[lo]:
                act(name)
            return
        size //= 4
        for q in range(lo, lo + 4 * size, size):
            @pl.when(lax.div(t, size) == q // size)
            def _(q=q):
                events(t, q, size)

    def run(t, before):
        events(t, 0, 64)
        code, add = pick(codes, t, 6), pick(adds, t, 6)
        adding(add, add_start)
        what, index = lax.div(code, 16), lax.rem(code, 16)
        for kind, body in ((TILE, tile), (ATT, attend), (UP, mlp_up), (DOWN, mlp_down)):
            @pl.when(what == kind)
            def _(body=body):
                body(index)

        adding(add, lambda s, kind, _: add_finish(s, kind))

        @pl.when(lax.div(before, 16) == DOWN)
        def _():
            own_stored(lax.rem(before, 16))

        return code

    lax.fori_loop(0, len(ORDER), run, jnp.int32(0))
    own_stored(jnp.int32(len(ITEMS) - 1))
    for name in LAST_ADDS:
        add_now(name)
    for k in range(len(ITEMS) - 2, len(ITEMS)):
        stage_free(jnp.int32(k))
    for s in range(3):
        for h in range(2):
            nm(s, h).wait_send()
            np_(s, h).wait_send()
            nf(s, h).wait_send()
        for i in range(6):
            nd(s, i).wait_send()
    for k in range(PIECES):
        wx(k).wait_send()
        for i in range(4):
            wf(k, i).wait_send()
    for s in range(3):
        from_part(s).wait_recv()
    for name, s in LAST_SUM.items():
        sent(s, BLOCKS.index(name))


def residual_kernel(x, branch, y, xv, bv, x_sem, b_sem, y_sem):
    parts, step = xv.shape[0], min(64, xv.shape[1])

    def loads(p):
        return (pltpu.make_async_copy(x.at[p], xv.at[p], x_sem.at[p]),
                pltpu.make_async_copy(branch.at[p], bv.at[p], b_sem.at[p]))

    def store(p):
        return pltpu.make_async_copy(xv.at[p], y.at[p], y_sem.at[p])

    for p in range(parts):
        for ld in loads(p):
            ld.start()

    def add(p, _):
        for ld in loads(p):
            ld.wait()
        for r in range(0, xv.shape[1], step):
            rr = pl.ds(r, step)
            xv[p, rr, :] = (xv[p, rr, :].astype(F32) + bv[p, rr, :].astype(F32)).astype(BF16)
        store(p).start()
        return 0

    lax.fori_loop(0, parts, add, 0)
    for p in range(parts):
        store(p).wait()


def neighbour_span(groups):
    short = 1
    while short * short * 4 <= groups:
        short *= 2
    return groups // short


def solution(mesh):
    tp, groups = mesh.shape["tp"], mesh.shape["dp"]
    span = neighbour_span(groups)
    assert tp == 8 and groups % (2 * span) == 0 and span % 2 == 0

    def local_layer(x_blk, ln_gain, ln_bias, w_qkv, w_out, w_up, w_down):
        n_seq, rows, d_model = x_blk.shape
        head = w_qkv.shape[3]
        ff = w_up.shape[1]
        ns, seq, blk = n_seq // 2, rows * tp, 2 * rows
        assert ns == 3 and w_qkv.shape[1:3] == (1, 3)
        chunk = min(512, d_model, ff)
        ln_rows, add_rows = min(64, rows // 2), min(16, rows // 2)
        dims = (span, rows, d_model, head, ff, chunk, ln_rows, add_rows)
        dma = pltpu.SemaphoreType.DMA
        anyspace = pl.BlockSpec(memory_space=pl.ANY)
        vmem = pl.BlockSpec(memory_space=pltpu.VMEM)

        def hbm(*shape):
            return jax.ShapeDtypeStruct(shape, BF16)

        outs = pl.pallas_call(
            functools.partial(layer_kernel, dims),
            name="layer",
            out_shape=(hbm(n_seq, rows, d_model), hbm(ns, seq, d_model), hbm(ns, rows, d_model), hbm(ns, seq, 2 * head),
                       hbm(ns, 4, rows, d_model), hbm(ns, 4, rows, d_model), hbm(ns, 2, rows, d_model)),
            in_specs=[anyspace, vmem, vmem, anyspace, anyspace, anyspace, anyspace],
            out_specs=(anyspace,) * 7,
            scratch_shapes=[
                pltpu.VMEM((3, d_model, 2 * head), BF16),
                pltpu.VMEM((d_model, 2 * ff), BF16),
                pltpu.VMEM((2 * ff + 2 * head, d_model), BF16),
                pltpu.VMEM((2, blk, d_model), BF16),
                pltpu.VMEM((2, blk, d_model), BF16),
                pltpu.VMEM((seq, 4 * head), BF16),
                pltpu.VMEM((2 * head, seq), BF16),
                pltpu.VMEM((2, blk, 2 * head), BF16),
                pltpu.VMEM((SLOTS, blk, 2 * ff + 2 * head), BF16),
                pltpu.VMEM((2, blk, d_model), BF16),
                pltpu.VMEM((3, rows, d_model), BF16),
                pltpu.VMEM((4, rows, d_model), BF16),
                pltpu.VMEM((2, head, blk), F32),
                pltpu.VMEM((2, 1, blk), F32),
                pltpu.VMEM((2, 1, blk), F32),
                dma((4,)), dma((PIECES,)), dma((PIECES,)), dma((PIECES, 4)), dma((PIECES, 4)),
                dma((ns, 2)), dma((ns, 2)), dma((ns, 2)), dma((ns, 2)), dma((ns, 2)), dma((ns, 2)),
                dma((ns, 6)), dma((ns, 6)),
                dma((ns, 4)), dma((ns, 4)), dma((2,)), dma((ns, 2)), dma((ns, 2)), dma((ns,)), dma((ns,)),
                dma((6,)), dma((2,)), dma((2,)), dma((2,)), dma((SLOTS,)), dma((3,)), dma,
            ],
            compiler_params=pltpu.CompilerParams(
                collective_id=0, has_side_effects=True, vmem_limit_bytes=VMEM_LIMIT),
        )(x_blk, ln_gain.reshape(1, d_model), ln_bias.reshape(1, d_model),
          jnp.transpose(w_qkv[:, 0], (1, 0, 2)), w_out, w_up, w_down)
        cut = (4 * n_seq, rows // 4, d_model)
        y = pl.pallas_call(
            residual_kernel, name="residual", in_specs=[anyspace, anyspace], out_specs=anyspace,
            out_shape=hbm(*cut),
            scratch_shapes=[pltpu.VMEM(cut, BF16), pltpu.VMEM(cut, BF16), dma(cut[:1]), dma(cut[:1]), dma(cut[:1])],
            compiler_params=pltpu.CompilerParams(vmem_limit_bytes=VMEM_LIMIT),
        )(x_blk.reshape(cut), outs[0].reshape(cut))
        return y.reshape(n_seq, rows, d_model)

    return jax.shard_map(
        local_layer, mesh=mesh,
        in_specs=(P("dp", "tp", None), P(), P(), P(None, "tp", None, None),
                  P("tp", None), P(None, "tp"), P("tp", None)),
        out_specs=P("dp", "tp", None), check_vma=False)
```

profile of v0, /device:TPU:81, one launch (start us, length us, event | category | flops | bytes accessed | tf_op | source)
XLA Modules:
  0.0 304.7 jit_solution(129796686205735875)
XLA Ops:
  0.0 296.9 %layer.1 = (bf16[6,256,2048]{2,1,0:T(8,128)(2,1)}, bf16[3,2048,2048]{2,1,0:T(8,128)(2,1)}, bf16[3,256,2048]{2,1,0:T(8,128)(2,1)}, bf16[3,2048,512]{2,1,0:T(8,128...) custom-call(bf16[6,256,2048]{2,1,0:T(8,128)(2,1)} %x.1, ...), custom_call_target="tpu_custom_call" | custom-call | tf_op jit(solution)/shard_map/layer/pallas_call | solution.py:705
  296.9 7.7 %residual.1 = bf16[24,64,2048]{2,1,0:T(8,128)(2,1)} custom-call(bf16[24,64,2048]{2,1,0:T(8,128)(2,1)} %bitcast.8, bf16[24,64,2048]{2,1,0:T(8,128)(2,1)} %bitcast.9), custom_call_target="tpu_custom_call" | custom-call | tf_op jit(solution)/shard_map/residual/pallas_call | solution.py:739
where the time goes:
time: 306 us; the launch traced here: 305 us
  Pallas kernels  305 us (100%)
    pallas_call x1, Pallas kernels, local_layer(): pl.pallas_call(functools.partial(layer_kernel, dims), name='layer', out_s...  297 us
    pallas_call x1, Pallas kernels, local_layer(): pl.pallas_call(residual_kernel, name='residual', in_specs=[anyspace, anys...  7.72 us

commit v1 on v0

--- a/solution.py
+++ b/solution.py
@@ -92,12 +92,11 @@
         seq += [(name[2:], t) for name in BEFORE.get(t, ()) if name[:2] == "ad"]
         if t in ADDS:
             seq.append((ADDS[t], t))
-    seq += [(name, None) for name in LAST_ADDS]
     last, before = {}, {}
     for name, _ in seq:
         before[name] = last.get(name[1], -1)
         last[name[1]] = int(name[0])
-    assert len(seq) == len(ITEMS)
+    assert len(seq) == len(ITEMS) - 1 and LAST_ADDS == ("2O",)
     return before, last
 
 
@@ -625,8 +624,8 @@
 
     lax.fori_loop(0, len(ORDER), run, jnp.int32(0))
     own_stored(jnp.int32(len(ITEMS) - 1))
-    for name in LAST_ADDS:
-        add_now(name)
+    remote(sibin.at[2, OWN], sibin.at[2, OWN], sp_s.at[2, OWN], sp_r.at[2, OWN], sib).wait_recv()
+    from_mate(2, MATE).wait_recv()
     for k in range(len(ITEMS) - 2, len(ITEMS)):
         stage_free(jnp.int32(k))
     for s in range(3):
@@ -646,32 +645,67 @@
         sent(s, BLOCKS.index(name))
 
 
-def residual_kernel(x, branch, y, xv, bv, x_sem, b_sem, y_sem):
-    parts, step = xv.shape[0], min(64, xv.shape[1])
-
-    def loads(p):
-        return (pltpu.make_async_copy(x.at[p], xv.at[p], x_sem.at[p]),
-                pltpu.make_async_copy(branch.at[p], bv.at[p], b_sem.at[p]))
-
-    def store(p):
-        return pltpu.make_async_copy(xv.at[p], y.at[p], y_sem.at[p])
-
-    for p in range(parts):
-        for ld in loads(p):
-            ld.start()
+def residual_kernel(x, branch, own, other, mate, y, xv, bv, ov, mv, x_sem, b_sem, o_sem, m_sem, y_sem):
+    n_seq, cuts, rows, _ = xv.shape
+    late = n_seq - 2 + lax.div(lax.axis_index("tp"), 4)
+
+    def at(ref, i):
+        return ref.at[pl.ds(pl.multiple_of(i * rows, rows), rows)]
+
+    def load_x(q, i):
+        return pltpu.make_async_copy(at(x.at[q], i), xv.at[q, i], x_sem.at[q, i])
+
+    def load_b(q, i):
+        return pltpu.make_async_copy(at(branch.at[q], i), bv.at[q, i], b_sem.at[q, i])
+
+    def load_late(i):
+        return (pltpu.make_async_copy(at(own.at[2, OWN], i), bv.at[late, i], b_sem.at[late, i]),
+                pltpu.make_async_copy(at(other.at[2, OWN], i), ov.at[i], o_sem.at[i]),
+                pltpu.make_async_copy(at(mate.at[2, MATE], i), mv.at[i], m_sem.at[i]))
+
+    def store(q, i):
+        return pltpu.make_async_copy(xv.at[q, i], at(y.at[q], i), y_sem.at[q, i])
+
+    def start(p, _):
+        q, i = lax.div(p, cuts), lax.rem(p, cuts)
+        load_x(q, i).start()
+
+        @pl.when(q == late)
+        def _():
+            for ld in load_late(i):
+                ld.start()
+
+        @pl.when(q != late)
+        def _():
+            load_b(q, i).start()
+
+        return 0
 
     def add(p, _):
-        for ld in loads(p):
-            ld.wait()
-        for r in range(0, xv.shape[1], step):
-            rr = pl.ds(r, step)
-            xv[p, rr, :] = (xv[p, rr, :].astype(F32) + bv[p, rr, :].astype(F32)).astype(BF16)
-        store(p).start()
+        q, i = lax.div(p, cuts), lax.rem(p, cuts)
+        load_x(q, i).wait()
+
+        @pl.when(q == late)
+        def _():
+            for ld in load_late(i):
+                ld.wait()
+            total = bv[q, i].astype(F32) + ov[i].astype(F32) + mv[i].astype(F32)
+            xv[q, i] = (xv[q, i].astype(F32) + total.astype(BF16).astype(F32)).astype(BF16)
+
+        @pl.when(q != late)
+        def _():
+            load_b(q, i).wait()
+            xv[q, i] = (xv[q, i].astype(F32) + bv[q, i].astype(F32)).astype(BF16)
+
+        store(q, i).start()
         return 0
 
-    lax.fori_loop(0, parts, add, 0)
-    for p in range(parts):
-        store(p).wait()
+    def done(p, _):
+        store(lax.div(p, cuts), lax.rem(p, cuts)).wait()
+        return 0
+
+    for step in (start, add, done):
+        lax.fori_loop(0, n_seq * cuts, step, 0)
 
 
 def neighbour_span(groups):
@@ -735,14 +769,15 @@
                 collective_id=0, has_side_effects=True, vmem_limit_bytes=VMEM_LIMIT),
         )(x_blk, ln_gain.reshape(1, d_model), ln_bias.reshape(1, d_model),
           jnp.transpose(w_qkv[:, 0], (1, 0, 2)), w_out, w_up, w_down)
-        cut = (4 * n_seq, rows // 4, d_model)
-        y = pl.pallas_call(
-            residual_kernel, name="residual", in_specs=[anyspace, anyspace], out_specs=anyspace,
-            out_shape=hbm(*cut),
-            scratch_shapes=[pltpu.VMEM(cut, BF16), pltpu.VMEM(cut, BF16), dma(cut[:1]), dma(cut[:1]), dma(cut[:1])],
+        cut = (n_seq, 4, rows // 4, d_model)
+        return pl.pallas_call(
+            residual_kernel, name="residual", in_specs=[anyspace] * 5, out_specs=anyspace,
+            out_shape=hbm(n_seq, rows, d_model),
+            scratch_shapes=[pltpu.VMEM(cut, BF16), pltpu.VMEM(cut, BF16), pltpu.VMEM(cut[1:], BF16),
+                            pltpu.VMEM(cut[1:], BF16), dma(cut[:2]), dma(cut[:2]), dma(cut[1:2]), dma(cut[1:2]),
+                            dma(cut[:2])],
             compiler_params=pltpu.CompilerParams(vmem_limit_bytes=VMEM_LIMIT),
-        )(x_blk.reshape(cut), outs[0].reshape(cut))
-        return y.reshape(n_seq, rows, d_model)
+        )(x_blk, outs[0], outs[4], outs[5], outs[6])
 
     return jax.shard_map(
         local_layer, mesh=mesh,

time: 306 us -> 307 us (level)
  no operation moved by 1% of the time
where the time goes in v1:
time: 307 us; the launch traced here: 305 us
  Pallas kernels  305 us (99%)
    pallas_call x1, Pallas kernels, local_layer(): pl.pallas_call(functools.partial(layer_kernel, dims), name='layer', out_s...  297 us
    pallas_call x1, Pallas kernels, local_layer(): pl.pallas_call(residual_kernel, name='residual', in_specs=[anyspace] * 5,...  8.43 us

profile of v1, /device:TPU:81, one launch (start us, length us, event | category | flops | bytes accessed | tf_op | source)
XLA Modules:
  0.0 305.3 jit_solution(7217217328698038875)
XLA Ops:
  0.0 296.9 %layer.1 = (bf16[6,256,2048]{2,1,0:T(8,128)(2,1)}, bf16[3,2048,2048]{2,1,0:T(8,128)(2,1)}, bf16[3,256,2048]{2,1,0:T(8,128)(2,1)}, bf16[3,2048,512]{2,1,0:T(8,128...) custom-call(bf16[6,256,2048]{2,1,0:T(8,128)(2,1)} %x.3, ...), custom_call_target="tpu_custom_call" | custom-call | tf_op jit(solution)/shard_map/layer/pallas_call | solution.py:739
  296.9 8.4 %residual.1 = bf16[6,256,2048]{2,1,0:T(8,128)(2,1)} custom-call(bf16[6,256,2048]{2,1,0:T(8,128)(2,1)} %x.3, bf16[6,256,2048]{2,1,0:T(8,128)(2,1)} %get-tuple-element.9.branch, bf16[3,4,256,2048]{3,2,1,0:T(8,128)(2,1)} %get-tuple-element.10.own, bf16[3,4,256,2048]{3,2,1,0:T(8,128)(2,1)} %get-tuple-element.11.other, ...), custom_call_target="tpu_custom_call" | custom-call | tf_op jit(solution)/shard_map/residual/pallas_call | solution.py:773

commit v2 on v0

--- a/solution.py
+++ b/solution.py
@@ -18,46 +18,48 @@
 PIECES = 10
 FAR, MATE, PART, OWN = range(4)
 TILE, ATT, UP, DOWN = range(4)
-INTER = ("Q2", "Q1", "Q0", "p01", "p00", "U0", "U1", "D2", "p11", "p10", "D0", "O", "D1", "D3", "p20", "p21")
-ORDER = ("A00", "A01", "A02", "A03", "T00", "T01", "T02", "T03", "A10", "A11", "U0F", "U1M",
-         "U0M", "A12", "A13", "T10", "T11", "T12", "T13", "A20", "D0F", "A21", "D1M", "U1F",
-         "D0M", "A22", "U0P", "D1F", "A23", "T20", "D0P", "T21", "T22", "T23", "U2F", "D2F",
-         "U1P", "D1P", "U2M", "D2M", "U2P", "U1O", "D2P", "D1O", "U0O", "D0O", "U2O", "D2O",
+INTER = ("Q2", "Q1", "Q0", "p00", "p01", "D0", "U1", "U0", "p11", "p10", "D3", "D1", "O", "D2", "p20", "p21")
+ORDER = ("A00", "A01", "A02", "A03", "T00", "T01", "T02", "T03", "A10", "A11", "U0F", "A12",
+         "U0M", "U1M", "A13", "T10", "T11", "T12", "T13", "U0P", "D0F", "U1F", "D0M", "D1M",
+         "A20", "A21", "A22", "U1P", "D0P", "D1F", "A23", "T20", "T21", "T22", "T23", "D1P",
+         "U2F", "D2F", "U2M", "U2P", "D2M", "U1O", "D2P", "D1O", "U0O", "D0O", "U2O", "D2O",
          )
-START = ("pqQ2", "pqQ1", "phQ2", "pqQ0", "phQ1", "rm0", "nm10", "phQ0", "rp01")
+START = ("pqQ2", "pqQ1", "phQ2", "pqQ0", "phQ1", "rm0", "nm10", "phQ0", "rp00")
 BEFORE = {
     0: ("ld00", "ld01"),
-    2: ("rp00", "ld02"),
-    3: ("pqU0", "rf0", "nm11", "pqU1", "ld03", "ln0"),
-    4: ("phU0", "pqD2"),
-    5: ("nm20",),
-    6: ("rm1",),
-    7: ("phU1", "ld10"),
-    8: ("rp11", "ld11"),
-    10: ("phD2", "rp10", "ln1", "ow0", "lo0"),
-    11: ("pqD0", "ln2"),
-    12: ("pqO", "ld12", "lo2"),
-    13: ("phD0", "pqD1", "rf1", "nm21"),
-    14: ("ld13", "ln3"),
-    15: ("pqD3", "phO"),
-    18: ("phD1", "rm2", "rp20", "ld20"),
-    19: ("phD3", "ow1", "lo1"),
-    20: ("rp21", "ld21"),
+    2: ("rp01", "pqD0", "ld02"),
+    3: ("phD0", "pqU1", "nm11", "rf0", "ld03", "ln0"),
+    4: ("pqU0", "nm20"),
+    6: ("phU1", "rm1"),
+    7: ("ld10",),
+    8: ("phU0", "rp11", "ld11"),
+    10: ("rp10", "ln1", "ow0", "lo0"),
+    11: ("pqD3", "ld12"),
+    12: ("pqD1", "ln2", "lo1"),
+    13: ("phD3", "pqO", "rf1", "nm21", "ln3"),
+    14: ("ld13",),
+    15: ("phD1", "pqD2"),
+    17: ("rm2",),
+    18: ("phO", "rp20"),
+    19: ("phD2", "ln4", "ow1", "lo2", "lo3"),
+    20: ("rp21",),
+    21: ("ln5", "lo4"),
     22: ("ad0F",),
-    23: ("rf2", "ln4", "lo3"),
-    24: ("ld22",),
-    26: ("lo4",),
-    27: ("ld23",),
-    28: ("ln5",),
-    34: ("ln6", "ow2", "lo5"),
-    36: ("ln7", "lo6"),
+    23: ("rf2", "ld20"),
+    24: ("ld21",),
+    25: ("ld22",),
+    27: ("lo5",),
+    29: ("ld23",),
+    30: ("ln6",),
+    36: ("ln7", "ow2", "lo6"),
     38: ("ln8", "lo7"),
-    40: ("ln9", "lo8"),
+    39: ("ln9", "lo8"),
     41: ("ln10", "lo9"),
     44: ("ln11", "lo10"),
+    45: ("ad2P",),
     46: ("lo11",),
 }
-ADDS = { 24: "1M", 29: "1F", 32: "0P", 33: "0M", 37: "2F", 39: "1P", 41: "2M", 44: "2P", 45: "1O", 47: "0O" }
+ADDS = { 24: "0M", 30: "0P", 31: "1F", 32: "1M", 37: "1P", 39: "2F", 42: "2M", 45: "1O", 47: "0O" }
 LAST_ADDS = ("2O",)
 
 KINDS = "ATUD"
@@ -592,29 +594,25 @@
                 def _(kind=kind):
                     do(lax.div(which, 4), kind, lax.div(code - 1, 12) - 1)
 
-    def events(t, lo, size):
-        if not any(p in BEFORE for p in range(lo, lo + size)):
+    def events(t, lo, hi):
+        if not any(p in BEFORE for p in range(lo, hi)):
             return
-        if size == 1:
+        if hi - lo == 1:
             for name in BEFORE[lo]:
                 act(name)
             return
-        size //= 4
-        for q in range(lo, lo + 4 * size, size):
-            @pl.when(lax.div(t, size) == q // size)
-            def _(q=q):
-                events(t, q, size)
+        half_way = (lo + hi) // 2
+        lax.cond(t < half_way, lambda: events(t, lo, half_way), lambda: events(t, half_way, hi))
 
     def run(t, before):
-        events(t, 0, 64)
+        events(t, 0, len(ORDER))
         code, add = pick(codes, t, 6), pick(adds, t, 6)
         adding(add, add_start)
         what, index = lax.div(code, 16), lax.rem(code, 16)
-        for kind, body in ((TILE, tile), (ATT, attend), (UP, mlp_up), (DOWN, mlp_down)):
-            @pl.when(what == kind)
-            def _(body=body):
-                body(index)
-
+        lax.cond(
+            what < UP,
+            lambda: lax.cond(what == TILE, lambda: tile(index), lambda: attend(index)),
+            lambda: lax.cond(what == UP, lambda: mlp_up(index), lambda: mlp_down(index)))
         adding(add, lambda s, kind, _: add_finish(s, kind))
 
         @pl.when(lax.div(before, 16) == DOWN)

time: 306 us -> 310 us (1.013)
  Pallas kernels: 305 us -> 310 us
    pallas_call x1, Pallas kernels: 297 us -> 302 us  [local_layer(): pl.pallas_call(functools.partial(layer_kernel, dims), name='layer', out_s...]
where the time goes in v2:
time: 310 us
  Pallas kernels  310 us (100%)
    pallas_call x1, Pallas kernels, local_layer(): pl.pallas_call(functools.partial(layer_kernel, dims), name='layer', out_s...  302 us
    pallas_call x1, Pallas kernels, local_layer(): pl.pallas_call(residual_kernel, name='residual', in_specs=[anyspace, anys...  7.72 us

profile of v2, /device:TPU:81, one launch (start us, length us, event | category | flops | bytes accessed | tf_op | source)
XLA Modules:
  0.0 309.6 jit_solution(8503300758431228225)
XLA Ops:
  0.0 301.9 %layer.1 = (bf16[6,256,2048]{2,1,0:T(8,128)(2,1)}, bf16[3,2048,2048]{2,1,0:T(8,128)(2,1)}, bf16[3,256,2048]{2,1,0:T(8,128)(2,1)}, bf16[3,2048,512]{2,1,0:T(8,128...) custom-call(bf16[6,256,2048]{2,1,0:T(8,128)(2,1)} %x.1, ...), custom_call_target="tpu_custom_call" | custom-call | tf_op jit(solution)/shard_map/layer/pallas_call | solution.py:703
  301.9 7.7 %residual.1 = bf16[24,64,2048]{2,1,0:T(8,128)(2,1)} custom-call(bf16[24,64,2048]{2,1,0:T(8,128)(2,1)} %bitcast.8, bf16[24,64,2048]{2,1,0:T(8,128)(2,1)} %bitcast.9), custom_call_target="tpu_custom_call" | custom-call | tf_op jit(solution)/shard_map/residual/pallas_call | solution.py:737
